TPU v7x, 32 devices: a whole 2x2x4 slice. The times are simulated.
32 devices in a mesh: dom: 8 (over y, x, core), tp: 4 (over z).
Axes of the slice: x: 2, y: 2, z: 4, core: 2. Of those that a mesh axis runs over, the one named last changes fastest.
Arguments:
- activations: bfloat16 [4, 128, 4096], P(None, 'dom', 'tp'), may hold values from -6 to 6
- norm_gain: float32 [4096], replicated, may hold values from 0.5 to 1.5
- w_query: bfloat16 [4096, 4096], P(None, 'tp'), may hold values from -0.09375 to 0.09375
- w_key: bfloat16 [4096, 1024], P(None, 'tp'), may hold values from -0.09375 to 0.09375
- value_weight: bfloat16 [4096, 1024], P(None, 'tp'), may hold values from -0.5 to 0.5
- w_output: bfloat16 [4096, 4096], P('tp'), may hold values from -0.09375 to 0.09375
- cache_keys: bfloat16 [128, 128, 1024], P('dom', None, 'tp'), may hold values from -740 to 740
- cache_values: bfloat16 [128, 128, 1024], P('dom', None, 'tp'), may hold values from -48 to 48
- tokens: int32 [4, 128], P(None, 'dom'), may hold values from 0 to 128255
- twisting_table: bfloat16 [128256], replicated, may hold values from -6 to 6
- twist_vec: float32 [4096], P('tp'), may hold values from -0.09375 to 0.09375
- previous_log_weights: float32 [128], P('dom'), may hold values from -300 to 0
- copy_counts: int32 [128], P('dom'), may hold values from 0 to 4, as said below
Outputs:
- attn_out: bfloat16 [4, 128, 4096], P(None, 'dom', 'tp')
- new_keys: bfloat16 [128, 132, 1024], P('dom', None, 'tp')
- new_values: bfloat16 [128, 132, 1024], P('dom', None, 'tp')
- out_logw: float32 [128], P('dom')
Inputs may be any that keep to these rules, and one draw needn't show every extreme that they name: copy_counts sum to 128; the particles of one index of dom have together at most 64 copies, and one index has exactly that many.
All inputs are finite; a program needn't handle non-finite values.
Results may differ from a plain program's by a relative error of at most 0.012.
The roundings to bfloat16 on the way count: a program that leaves them out, or rounds other values in their place, can miss the bound.
Values may be sent and summed in bfloat16 or wider, within the bound.
A program may use at most 128 MiB of HBM per device.

v0:
```python
import jax
import jax.numpy as jnp
from jax import lax
from jax.sharding import PartitionSpec as P

D = 4096
HD = 128


def entering(part, axis, combine, identity):
    place = lax.axis_index(axis)
    gathered = lax.all_gather(part, axis)
    state = jnp.zeros_like(part) + jnp.asarray(identity, part.dtype)

    def one(lap, state):
        return combine(state, lax.dynamic_index_in_dim(gathered, lap, 0, False))

    return lax.fori_loop(0, place, one, state)


def rotate(tensor, positions):
    middle = tensor.shape[-1] // 2
    frequency = 500000.0 ** (-2.0 * jnp.arange(middle, dtype=jnp.float32) / tensor.shape[-1])
    angles = positions[:, None] * frequency[None, :]
    cosine = jnp.cos(angles)[:, None, None, :]
    sine_part = jnp.sin(angles)[:, None, None, :]
    lower_half = tensor[..., :middle]
    upper_half = tensor[..., middle:]
    return jnp.concatenate(
        [
            lower_half * cosine - upper_half * sine_part,
            upper_half * cosine + lower_half * sine_part,
        ],
        -1,
    )


def add_counts(former, latter):
    return former + latter


def local(
    activations,
    norm_gain,
    w_query,
    w_key,
    value_weight,
    w_output,
    cache_keys,
    cache_values,
    tokens,
    twisting_table,
    twist_vec,
    previous_log_weights,
    copy_counts,
):
    step_count = activations.shape[0]
    particle_count = activations.shape[1]
    span_old = cache_keys.shape[1]
    dom_size = lax.axis_size("dom")
    kv_local = w_key.shape[1] // HD
    q_local = w_query.shape[1] // HD
    group_size = q_local // kv_local
    capacity = 4 * particle_count // dom_size
    total_copies = jnp.sum(copy_counts)
    offset = entering(total_copies, "dom", add_counts, jnp.int32(0))
    starts = jnp.cumsum(copy_counts) - copy_counts
    position = jnp.arange(dom_size * capacity, dtype=jnp.int32)
    target = position // capacity
    copy_rank = position % capacity * dom_size + (target - offset) % dom_size
    is_live = copy_rank < total_copies
    source = jnp.sum((starts[None, :] <= copy_rank[:, None]).astype(jnp.int32), 1) - 1
    arrival = jnp.where(is_live, (offset + copy_rank) // dom_size, particle_count).astype(
        jnp.bfloat16
    )

    def pack_rows(tensor):
        return jnp.where(is_live[:, None, None], tensor[source], jnp.zeros((), tensor.dtype))

    def place_rows(tensor, slot_index):
        blank = jnp.zeros((particle_count,) + tensor.shape[1:], tensor.dtype)
        return blank.at[slot_index].set(tensor, mode="drop")

    gathered = lax.all_gather(activations, "tp", axis=2, tiled=True)
    inputs = gathered.astype(jnp.float32)
    normed = (
        inputs * lax.rsqrt(jnp.mean(inputs * inputs, -1, keepdims=True) + 1e-05) * norm_gain
    ).astype(jnp.bfloat16)
    flat_rows = normed.reshape(step_count * particle_count, D)
    positions = (span_old + jnp.arange(step_count, dtype=jnp.int32)).astype(jnp.float32)
    queries = jnp.dot(flat_rows, w_query, preferred_element_type=jnp.float32).reshape(
        step_count, particle_count, q_local, HD
    )
    queries = rotate(queries, positions).astype(jnp.bfloat16)
    fresh_keys = jnp.dot(flat_rows, w_key, preferred_element_type=jnp.float32).reshape(
        step_count, particle_count, kv_local, HD
    )
    fresh_keys = (
        rotate(fresh_keys, positions)
        .astype(jnp.bfloat16)
        .reshape(step_count, particle_count, kv_local * HD)
    )
    fresh_values = jnp.dot(flat_rows, value_weight, preferred_element_type=jnp.float32).astype(
        jnp.bfloat16
    )
    fresh_values = fresh_values.reshape(step_count, particle_count, kv_local * HD)
    fresh_keys = jnp.transpose(fresh_keys, (1, 0, 2))
    fresh_values = jnp.transpose(fresh_values, (1, 0, 2))
    key_rows = jnp.concatenate([cache_keys, fresh_keys], 1)
    value_rows = jnp.concatenate([cache_values, fresh_values], 1)
    key_span = span_old + step_count
    query_heads = queries.reshape(step_count, particle_count, kv_local, group_size, HD)
    key_heads = key_rows.reshape(particle_count, key_span, kv_local, HD)
    value_heads = value_rows.reshape(particle_count, key_span, kv_local, HD)
    scores = (
        jnp.einsum("snkgd,nlkd->snkgl", query_heads, key_heads, preferred_element_type=jnp.float32)
        / HD**0.5
    )
    allowed = (
        jnp.arange(key_span, dtype=jnp.int32)[None, :]
        <= (span_old + jnp.arange(step_count, dtype=jnp.int32))[:, None]
    )
    allowed = allowed[:, None, None, None, :]
    masked = jnp.where(allowed, scores, -jnp.inf)
    highest = jnp.max(masked, -1, keepdims=True)
    exponent = jnp.exp(masked - highest)
    weights = (exponent / jnp.sum(exponent, -1, keepdims=True)).astype(jnp.bfloat16)
    context = jnp.einsum(
        "snkgl,nlkd->snkgd", weights, value_heads, preferred_element_type=jnp.float32
    ).astype(jnp.bfloat16)
    context = context.reshape(step_count * particle_count, q_local * HD)
    partial_value = jnp.dot(context, w_output, preferred_element_type=jnp.float32).reshape(
        step_count, particle_count, D
    )
    head_mix = lax.psum_scatter(partial_value, "tp", scatter_dimension=2, tiled=True)
    attn_out = head_mix.astype(jnp.bfloat16)
    summed = activations.astype(jnp.float32) + head_mix
    aligned, energy = lax.psum(
        (jnp.sum(summed * twist_vec, -1), jnp.sum(summed * summed, -1)), "tp"
    )
    twisting_score = aligned / jnp.sqrt(energy / D + 1e-06)
    token_reward = twisting_table[tokens].astype(jnp.float32)
    particle_log_weight = previous_log_weights + jnp.sum(token_reward + twisting_score, 0)
    largest = lax.pmax(jnp.max(particle_log_weight), "dom")
    mass_total = lax.psum(jnp.sum(jnp.exp(particle_log_weight - largest)), "dom")
    out_logw = particle_log_weight - (largest + jnp.log(mass_total))
    moved_keys, moved_values, arrived = (
        lax.all_to_all(pack_rows(key_rows), "dom", split_axis=0, concat_axis=0, tiled=True),
        lax.all_to_all(pack_rows(value_rows), "dom", split_axis=0, concat_axis=0, tiled=True),
        lax.all_to_all(arrival, "dom", split_axis=0, concat_axis=0, tiled=True),
    )
    slot_index = arrived.astype(jnp.int32)
    new_keys = place_rows(moved_keys, slot_index)
    new_values = place_rows(moved_values, slot_index)
    return (attn_out, new_keys, new_values, out_logw)


def solution(mesh):
    return jax.shard_map(
        local,
        mesh=mesh,
        in_specs=(
            P(None, "dom", "tp"),
            P(),
            P(None, "tp"),
            P(None, "tp"),
            P(None, "tp"),
            P("tp", None),
            P("dom", None, "tp"),
            P("dom", None, "tp"),
            P(None, "dom"),
            P(),
            P("tp"),
            P("dom"),
            P("dom"),
        ),
        out_specs=(P(None, "dom", "tp"), P("dom", None, "tp"), P("dom", None, "tp"), P("dom")),
        check_vma=False,
    )
```

profile of v0, /device:TPU:0, one launch (start us, length us, event | category | flops | bytes accessed | tf_op | source)
XLA Modules:
  0.0 234.3 jit_solution(9963035594114682076)
XLA Ops:
  7.2 0.9 copy.65
  8.1 0.1 reduce.1
  8.2 1.3 fusion.34
  9.5 1.2 dynamic-slice
  10.8 1.4 dynamic-update-slice
  12.2 9.5 %all-reduce = s32[8]{0:T(128)S(1)} all-reduce(s32[8]{0:T(128)S(1)} %dynamic-update-slice), channel_id=1, replica_groups=mesh['dom'=8,'tp'=4] {'dom'}, use_global_device_ids=true, to_apply=%add | all-reduce | flops 8 | bytes 64
  21.7 1.3 fusion.23
  22.9 10.4 %all-to-all-start = ((bf16[8,8,1]{1,2,0:T(2,128)(2,1)}), bf16[8,8,1]{1,2,0:T(2,128)(2,1)S(1)}, u32[]{:S(2)}, u32[]{:S(2)}) async-start(bf16[8,8,1]{1,2,0:T(2,128)(2,1)} %fusion.23), calls=%async_computation.1 | async-start | bytes 8192 | tf_op jit(solution)/shard_map/all_to_all | solution.py:150
  33.4 0.7 broadcast_compare_fusion
  34.0 16.7 %all_gather.9 = bf16[4,16,4096]{2,1,0:T(8,128)(2,1)S(1)} all-gather(bf16[4,16,1024]{2,1,0:T(8,128)(2,1)} %param.15), channel_id=1, replica_groups=mesh['dom'=8,'tp'=4] {'tp'}, dimensions={2}, use_global_device_ids=true | all-gather | bytes 655360 | tf_op jit(solution)/shard_map/all_gather | solution.py:84
  50.7 0.2 fusion.10
  50.9 4.1 %copy.75 = bf16[256,4096]{1,0:T(8,128)(2,1)} copy(bf16[256,4096]{0,1:T(8,128)(2,1)} %bitcast.59) | data formatting | bytes 4194304 | tf_op jit(solution)/shard_map/dot_general | solution.py:95
  55.1 0.2 fusion.12
  55.3 2.5 %fusion.15 = f32[4,16,2,128]{3,1,2,0:T(8,128)S(1)} fusion(bf16[2,128,4096,1]{2,1,0,3:T(8,128)(2,1)} %bitcast.60, bf16[4,16,4096]{2,1,0:T(8,128)(2,1)S(1)} %fusion.12), kind=kOutput, calls=%fused_computation.29 | convolution fusion | flops 134217728 | bytes 2686976 | tf_op jit(solution)/shard_map/dot_general | solution.py:95
  57.8 0.1 multiply_cosine_fusion
  57.9 0.1 subtract_convert_fusion.1
  58.0 0.1 pad_maximum_fusion.2
  58.2 0.5 convolution_convert_fusion.1
  58.7 0.1 convert_reduce_fusion
  58.8 0.6 copy-done.6
  59.5 0.2 copy-done.7
  59.8 2.9 %gather_fusion = bf16[64,132,256]{2,1,0:T(8,128)(2,1)} fusion(bf16[16,132,256]{2,1,0:T(8,128)(2,1)S(1)} %pad_maximum_fusion.1, s32[1024]{0:T(1024)S(1)} %pad_clamp_fusion.1), kind=kCustom, calls=%fused_computation | custom fusion | bytes 8651008 | tf_op jit(solution)/shard_map/gather | solution.py:78
  62.7 2.9 %gather_fusion.1 = bf16[64,132,256]{2,1,0:T(8,128)(2,1)} fusion(bf16[16,132,256]{2,1,0:T(8,128)(2,1)S(1)} %pad_maximum_fusion, s32[1024]{0:T(1024)S(1)} %pad_clamp_fusion.1), kind=kCustom, calls=%fused_computation.1 | custom fusion | bytes 8651008 | tf_op jit(solution)/shard_map/gather | solution.py:78
  65.6 7.6 %broadcast_select_fusion = (bf16[64,132,256]{2,1,0:T(8,128)(2,1)}, bf16[64,132,256]{2,1,0:T(8,128)(2,1)}) fusion(bf16[64,132,256]{2,1,0:T(8,128)(2,1)} %gather_fusion.1, pred[64]{0:T(512)(128)(4,1)S(1)} %broadcast_compare_fusion, bf16[64,132,256]{2,1,0:T(8,128)(2,1)} %gather_fusion), kind=kLoop, calls=%fused_computation.8 | loop fusion | flops 4325376 | bytes 17301568 | tf_op jit(solution)/shard_map/jit(_where)/select_n | solution.py:78
  73.2 4.6 %all-to-all-start.1 = ((bf16[64,132,256]{2,1,0:T(8,128)(2,1)}), bf16[64,132,256]{2,1,0:T(8,128)(2,1)}, u32[]{:S(2)}, u32[]{:S(2)}) async-start(bf16[64,132,256]{2,1,0:T(8,128)(2,1)} %get-tuple-element.62), calls=%async_computation.2 | async-start | bytes 8912896 | tf_op jit(solution)/shard_map/all_to_all | solution.py:148
  77.9 1.2 reshape.513
  79.0 0.4 reshape.511
  79.4 11.3 %copy.81 = bf16[1024,4096]{1,0:T(8,128)(2,1)} copy(bf16[1024,4096]{0,1:T(8,128)(2,1)} %bitcast.57) | data formatting | bytes 16777216 | tf_op jit(solution)/shard_map/dot_general | solution.py:91
  90.7 6.1 %fusion.13 = f32[4,16,8,128]{3,1,2,0:T(8,128)S(1)} fusion(bf16[8,128,4096,1]{2,1,0,3:T(8,128)(2,1)} %bitcast.58, bf16[4,16,4096]{2,1,0:T(8,128)(2,1)S(1)} %copy-done.4), kind=kOutput, calls=%fused_computation.27 | convolution fusion | flops 536870912 | bytes 9175040 | tf_op jit(solution)/shard_map/dot_general | solution.py:91
  96.9 0.2 subtract_convert_fusion
  97.2 1.8 fusion.35
  99.0 30.7 %all-to-all-done.1 = bf16[64,132,256]{2,1,0:T(8,128)(2,1)} async-done(((bf16[64,132,256]{2,1,0:T(8,128)(2,1)}), bf16[64,132,256]{2,1,0:T(8,128)(2,1)}, u32[]{:S(2)}, u32[]{:S(2)}) %all-to-all-start.1) | async-done | bytes 4325408 | tf_op jit(solution)/shard_map/all_to_all | solution.py:148
  129.8 4.7 %all-to-all-start.2 = ((bf16[64,132,256]{2,1,0:T(8,128)(2,1)}), bf16[64,132,256]{2,1,0:T(8,128)(2,1)}, u32[]{:S(2)}, u32[]{:S(2)}) async-start(bf16[64,132,256]{2,1,0:T(8,128)(2,1)} %get-tuple-element.61), calls=%async_computation.3 | async-start | bytes 8912896 | tf_op jit(solution)/shard_map/all_to_all | solution.py:149
  134.5 0.5 fusion.7
  135.1 6.0 %fusion.1 = f32[4,16,4096]{2,1,0:T(8,128)} fusion(bf16[4,16,1024]{2,1,0:T(8,128)(2,1)S(1)} %dot_general.37, bf16[1024,4096]{1,0:T(8,128)(2,1)} %param.20), kind=kOutput, calls=%fused_computation.6 | convolution fusion | flops 536870912 | bytes 9568256 | tf_op jit(solution)/shard_map/dot_general | solution.py:132
  141.3 0.8 gather_fusion.2
  142.3 27.8 %reduce-scatter.2.cloned.1.call-done = f32[4,16,1024]{2,1,0:T(8,128)} async-done(((f32[4,16,4096]{2,1,0:T(8,128)}), f32[4,16,1024]{2,1,0:T(8,128)}) %reduce-scatter.2.cloned.1.call-update) | async-done | bytes 262160 | tf_op jit(solution)/shard_map/reduce_scatter | solution.py:135
  170.1 1.8 multiply_reduce_fusion
  171.9 9.2 %all-reduce.1 = (f32[4,16]{1,0:T(4,128)S(1)}, f32[4,16]{1,0:T(4,128)S(1)}) all-reduce(f32[4,16]{1,0:T(4,128)S(1)} %get-tuple-element.41, f32[4,16]{1,0:T(4,128)S(1)} %get-tuple-element.40), channel_id=1, replica_groups=mesh['dom'=8,'tp'=4] {'tp'}, use_global_device_ids=true, to_apply=%region_12.13 | all-reduce | flops 128 | bytes 1024 | tf_op jit(solution)/shard_map/psum | solution.py:138
  181.1 0.6 fusion.33
  181.7 12.4 %pmax.7 = f32[]{:T(128)} all-reduce(f32[]{:T(128)} %get-tuple-element.52), channel_id=1, replica_groups=mesh['dom'=8,'tp'=4] {'dom'}, use_global_device_ids=true, to_apply=%region_17.18 | all-reduce | flops 1 | bytes 8 | tf_op jit(solution)/shard_map/pmax | solution.py:144
  194.2 1.2 exponential_reduce_fusion
  195.4 12.5 %psum.23 = f32[]{:T(128)} all-reduce(f32[]{:T(128)} %exponential_reduce_fusion), channel_id=1, replica_groups=mesh['dom'=8,'tp'=4] {'dom'}, use_global_device_ids=true, to_apply=%region_19.20 | all-reduce | flops 1 | bytes 8 | tf_op jit(solution)/shard_map/psum | solution.py:145
  209.2 0.5 broadcast_subtract_fusion
  209.8 7.6 %scatter_fusion = bf16[16,132,256]{2,1,0:T(8,128)(2,1)S(1)} fusion(bf16[16,132,256]{2,1,0:T(8,128)(2,1)S(1)} %broadcast.504.clone, s32[64]{0:T(128)S(1)} %fusion.29, bf16[64,132,256]{2,1,0:T(8,128)(2,1)} %all-to-all-done.1), kind=kCustom, calls=%fused_computation.3 | custom fusion | bytes 12976384 | tf_op jit(solution)/shard_map/scatter | solution.py:82
  217.4 1.2 copy.66
  218.7 7.6 %scatter_fusion.1 = bf16[16,132,256]{2,1,0:T(8,128)(2,1)S(1)} fusion(bf16[16,132,256]{2,1,0:T(8,128)(2,1)S(1)} %broadcast.504.clone.1, s32[64]{0:T(128)S(1)} %fusion.29, bf16[64,132,256]{2,1,0:T(8,128)(2,1)} %all-to-all-done.2), kind=kCustom, calls=%fused_computation.4 | custom fusion | bytes 12976384 | tf_op jit(solution)/shard_map/scatter | solution.py:82
  226.3 1.2 copy.67
  (60 shorter events, 1.2 us)
Async XLA Ops:
  7.2 51.0 %copy-start = (bf16[4096,256]{1,0:T(8,128)(2,1)S(1)}, bf16[4096,256]{1,0:T(8,128)(2,1)}, u32[]{:S(2)}) copy-start(bf16[4096,256]{1,0:T(8,128)(2,1)} %param.19) | copy-start | bytes 6291460
  22.9 50.3 %all-to-all-start = ((bf16[8,8,1]{1,2,0:T(2,128)(2,1)}), bf16[8,8,1]{1,2,0:T(2,128)(2,1)S(1)}, u32[]{:S(2)}, u32[]{:S(2)}) async-start(bf16[8,8,1]{1,2,0:T(2,128)(2,1)} %fusion.23), calls=%async_computation.1 | async-start | bytes 8192 | tf_op jit(solution)/shard_map/all_to_all | solution.py:150
  50.9 4.2 %copy-start.9 = (f32[4096]{0:T(1024)S(1)}, f32[4096]{0:T(1024)}, u32[]{:S(2)}) copy-start(f32[4096]{0:T(1024)} %param.16) | copy-start | bytes 49156
  55.3 2.9 %copy-start.3 = (bf16[4,16,4096]{2,1,0:T(8,128)(2,1)}, bf16[4,16,4096]{2,1,0:T(8,128)(2,1)S(1)}, u32[]{:S(2)}) copy-start(bf16[4,16,4096]{2,1,0:T(8,128)(2,1)S(1)} %fusion.12) | copy-start | bytes 1572868
  58.2 1.2 copy-start.6
  58.2 1.5 copy-start.7
  73.2 56.5 %all-to-all-start.1 = ((bf16[64,132,256]{2,1,0:T(8,128)(2,1)}), bf16[64,132,256]{2,1,0:T(8,128)(2,1)}, u32[]{:S(2)}, u32[]{:S(2)}) async-start(bf16[64,132,256]{2,1,0:T(8,128)(2,1)} %get-tuple-element.62), calls=%async_computation.2 | async-start | bytes 8912896 | tf_op jit(solution)/shard_map/all_to_all | solution.py:148
  79.4 11.3 %copy-start.4 = (bf16[4,16,4096]{2,1,0:T(8,128)(2,1)S(1)}, bf16[4,16,4096]{2,1,0:T(8,128)(2,1)}, u32[]{:S(2)}) copy-start(bf16[4,16,4096]{2,1,0:T(8,128)(2,1)} %copy-done.3) | copy-start | bytes 1572868
  90.7 6.5 %copy-start.5 = (bf16[16,132,2,128]{3,2,1,0:T(2,128)(2,1)S(1)}, bf16[16,132,2,128]{3,2,1,0:T(2,128)(2,1)}, u32[]{:S(2)}) copy-start(bf16[16,132,2,128]{3,2,1,0:T(2,128)(2,1)} %reshape.513) | copy-start | bytes 3244036
  129.8 4.7 %copy-start.13 = (f32[4,16,2,4,132]{4,3,0,2,1:T(4,128)S(1)}, f32[4,16,2,4,132]{4,3,0,2,1:T(4,128)}, u32[]{:S(2)}) copy-start(f32[4,16,2,4,132]{4,3,0,2,1:T(4,128)} %get-tuple-element.66) | copy-start | bytes 811012
  129.8 88.8 %all-to-all-start.2 = ((bf16[64,132,256]{2,1,0:T(8,128)(2,1)}), bf16[64,132,256]{2,1,0:T(8,128)(2,1)}, u32[]{:S(2)}, u32[]{:S(2)}) async-start(bf16[64,132,256]{2,1,0:T(8,128)(2,1)} %get-tuple-element.61), calls=%async_computation.3 | async-start | bytes 8912896 | tf_op jit(solution)/shard_map/all_to_all | solution.py:149
  134.5 35.6 %reduce-scatter.2.cloned.1.call-start = ((), (), s32[]{:S(2)}) async-start(), calls=%async_computation.4 | async-start | bytes 1310720 | tf_op jit(solution)/shard_map/reduce_scatter | solution.py:135
  135.1 6.0 %copy-start.11 = (s32[4,16]{1,0:T(4,128)S(1)}, s32[4,16]{1,0:T(4,128)}, u32[]{:S(2)}) copy-start(s32[4,16]{1,0:T(4,128)} %param.23) | copy-start | bytes 772
  135.1 6.1 %copy-start.2 = (bf16[128256]{0:T(1024)(128)(2,1)S(1)}, bf16[128256]{0:T(1024)(128)(2,1)}, u32[]{:S(2)}) copy-start(bf16[128256]{0:T(1024)(128)(2,1)} %param.24) | copy-start | bytes 769540
  141.1 29.0 %copy-start.8 = (bf16[4,16,1024]{2,1,0:T(8,128)(2,1)S(1)}, bf16[4,16,1024]{2,1,0:T(8,128)(2,1)}, u32[]{:S(2)}) copy-start(bf16[4,16,1024]{2,1,0:T(8,128)(2,1)} %param.15) | copy-start | bytes 393220
  141.1 29.0 %copy-start.10 = (f32[1024]{0:T(1024)S(1)}, f32[1024]{0:T(1024)}, u32[]{:S(2)}) copy-start(f32[1024]{0:T(1024)} %param.25) | copy-start | bytes 12292
  141.1 40.0 %copy-start.12 = (f32[16]{0:T(128)S(1)}, f32[16]{0:T(128)}, u32[]{:S(2)}) copy-start(f32[16]{0:T(128)} %param.26) | copy-start | bytes 196
  218.7 8.8 %copy-start.1 = (bf16[4096,256]{1,0:T(8,128)(2,1)S(1)}, bf16[4096,256]{1,0:T(8,128)(2,1)}, u32[]{:S(2)}) copy-start(bf16[4096,256]{1,0:T(8,128)(2,1)} %param.19) | copy-start | bytes 6291460
Sparse Core Ops, SparseCore 0:
  141.3 28.7 reduce-scatter.1
where the time goes:
time: 236 us; the launch traced here: 234 us
  blocking collectives  60.3 us (26%)
  waiting for transfers between devices  58.6 us (25%)
  local copies, waits for them, and re-layouts  46.2 us (20%)
  starting transfers between devices  19.8 us (8%)
  matrix products  17.4 us (7%)
  other arithmetic  16.4 us (7%)
  between operations  15.7 us (7%)
    all_to_all x1, waiting for transfers between devices, local(): lax.all_to_all(pack_rows(key_rows), 'dom', split_axis=0, concat_axis=0, t...  30.7 us
    reduce_scatter x1, waiting for transfers between devices, local(): lax.psum_scatter(partial_value, 'tp', scatter_dimension=2, tiled=True)  27.8 us
    all_gather x1, blocking collectives, local(): gathered = lax.all_gather(activations, 'tp', axis=2, tiled=True)  16.7 us
    scatter x2, local copies, waits for them, and re-layouts, place_rows(): return blank.at[slot_index].set(tensor, mode='drop')  15.2 us
    psum x1, blocking collectives, local(): lax.psum(jnp.sum(jnp.exp(particle_log_weight - largest)), 'dom')  12.5 us
    pmax x1, blocking collectives, local(): largest = lax.pmax(jnp.max(particle_log_weight), 'dom')  12.4 us
    dot_general x1, local copies, waits for them, and re-layouts, local(): jnp.dot(flat_rows, w_query, preferred_element_type=jnp.float32)  11.3 us
    all_to_all x1, starting transfers between devices, local(): lax.all_to_all(arrival, 'dom', split_axis=0, concat_axis=0, tiled=True)  10.4 us
  transfers between devices with their start and end apart: 4, of which 2 were waited for; matrix products, arithmetic and copies ran while one was open for 27% of the time, Pallas kernels for 0%

commit v1 on v0

--- a/solution.py
+++ b/solution.py
@@ -81,7 +81,12 @@
         blank = jnp.zeros((particle_count,) + tensor.shape[1:], tensor.dtype)
         return blank.at[slot_index].set(tensor, mode="drop")
 
-    gathered = lax.all_gather(activations, "tp", axis=2, tiled=True)
+    ring = [activations]
+    for hop in range(3):
+        ring.append(lax.ppermute(ring[-1], "tp", [(dev, (dev + 1) % 4) for dev in range(4)]))
+    gathered = jnp.roll(
+        jnp.concatenate(ring[::-1], axis=2), (lax.axis_index("tp") + 1) * ring[0].shape[2], axis=2
+    )
     inputs = gathered.astype(jnp.float32)
     normed = (
         inputs * lax.rsqrt(jnp.mean(inputs * inputs, -1, keepdims=True) + 1e-05) * norm_gain

time: 236 us -> 229 us (0.970)
  blocking collectives: 60.3 us -> 42.2 us
  waiting for transfers between devices: 58.6 us -> 66.9 us
  starting transfers between devices: 19.8 us -> 24.4 us
  matrix products: 17.4 us -> 14.8 us
    all_gather x1 -> x0, blocking collectives: 16.7 us -> none  [local(): gathered = lax.all_gather(activations, 'tp', axis=2, tiled=True)]
    ppermute x0 -> x3, waiting for transfers between devices: none -> 8.02 us  [local(): lax.ppermute(ring[-1], 'tp', [(dev, (dev + 1) % 4) for dev in range(4)])]
    ppermute x0 -> x3, starting transfers between devices: none -> 4.74 us  [local(): lax.ppermute(ring[-1], 'tp', [(dev, (dev + 1) % 4) for dev in range(4)])]
    unnamed x33 -> x38, local copies, waits for them, and re-layouts: 5.91 us -> 6.1 us
  transfers between devices with their start and end apart: 4 -> 7, of which waited for: 2 -> 4; matrix products, arithmetic and copies ran while one was open for 27% -> 30% of each run, Pallas kernels for 0% -> 0%
where the time goes in v1:
time: 229 us; the launch traced here: 227 us
  waiting for transfers between devices  66.9 us (29%)
  local copies, waits for them, and re-layouts  46.2 us (20%)
  blocking collectives  42.2 us (18%)
  starting transfers between devices  24.4 us (11%)
  other arithmetic  17.1 us (7%)
  between operations  15.8 us (7%)
  matrix products  14.8 us (6%)
    all_to_all x1, waiting for transfers between devices, local(): lax.all_to_all(pack_rows(key_rows), 'dom', split_axis=0, concat_axis=0, t...  31.5 us
    reduce_scatter x1, waiting for transfers between devices, local(): lax.psum_scatter(partial_value, 'tp', scatter_dimension=2, tiled=True)  27.4 us
    scatter x2, local copies, waits for them, and re-layouts, place_rows(): return blank.at[slot_index].set(tensor, mode='drop')  15.2 us
    psum x1, blocking collectives, local(): lax.psum(jnp.sum(jnp.exp(particle_log_weight - largest)), 'dom')  12.5 us
    pmax x1, blocking collectives, local(): largest = lax.pmax(jnp.max(particle_log_weight), 'dom')  12.4 us
    dot_general x1, local copies, waits for them, and re-layouts, local(): jnp.dot(flat_rows, w_query, preferred_element_type=jnp.float32)  11.3 us
    all_to_all x1, starting transfers between devices, local(): lax.all_to_all(arrival, 'dom', split_axis=0, concat_axis=0, tiled=True)  10.4 us
    psum x1, blocking collectives, local(): lax.psum((jnp.sum(summed * twist_vec, -1), jnp.sum(summed * summed, -1)),...  9.26 us
  transfers between devices with their start and end apart: 7, of which 4 were waited for; matrix products, arithmetic and copies ran while one was open for 30% of the time, Pallas kernels for 0%

profile of v1, /device:TPU:0, one launch (start us, length us, event | category | flops | bytes accessed | tf_op | source)
XLA Modules:
  0.0 227.4 jit_solution(3006747422098504946)
XLA Ops:
  7.2 3.1 %collective-permute-start = (bf16[4,16,1024]{2,1,0:T(8,128)(2,1)}, bf16[4,16,1024]{2,1,0:T(8,128)(2,1)S(1)}, u32[]{:S(2)}, u32[]{:S(2)}) collective-permute-start(bf16[4,16,1024]{2,1,0:T(8,128)(2,1)} %param.15), channel_id=1, source_target_pairs={{0,1},{1,2},{2,3},{3,0},{4,5},{5,6},{6,7},{7,4},{8,9},{9,10},{10,1... | collective-permute-start | bytes 393224 | tf_op jit(solution)/shard_map/ppermute | solution.py:86
  10.3 0.7 copy.65
  11.1 0.1 reduce.1
  11.2 1.3 fusion.34
  12.5 1.2 dynamic-slice
  13.7 1.4 dynamic-update-slice
  15.1 8.0 %all-reduce = s32[8]{0:T(128)S(1)} all-reduce(s32[8]{0:T(128)S(1)} %dynamic-update-slice), channel_id=1, replica_groups=mesh['dom'=8,'tp'=4] {'dom'}, use_global_device_ids=true, to_apply=%add | all-reduce | flops 8 | bytes 64
  23.1 1.3 fusion.23
  24.4 10.4 %all-to-all-start = ((bf16[8,8,1]{1,2,0:T(2,128)(2,1)}), bf16[8,8,1]{1,2,0:T(2,128)(2,1)S(1)}, u32[]{:S(2)}, u32[]{:S(2)}) async-start(bf16[8,8,1]{1,2,0:T(2,128)(2,1)} %fusion.23), calls=%async_computation.1 | async-start | bytes 8192 | tf_op jit(solution)/shard_map/all_to_all | solution.py:155
  34.8 0.7 compare_select_fusion.9
  35.7 1.6 collective-permute-start.1
  37.4 6.1 %collective-permute-done.1 = bf16[4,16,1024]{2,1,0:T(8,128)(2,1)S(1)} collective-permute-done((bf16[4,16,1024]{2,1,0:T(8,128)(2,1)S(1)}, bf16[4,16,1024]{2,1,0:T(8,128)(2,1)S(1)}, u32[]{:S(2)}, u32[]{:S(2)}) %collective-permute-start.1) | collective-permute-done | bytes 131104 | tf_op jit(solution)/shard_map/ppermute | solution.py:86
  43.5 0.7 broadcast_compare_fusion
  44.2 4.2 %copy.75 = bf16[256,4096]{1,0:T(8,128)(2,1)} copy(bf16[256,4096]{0,1:T(8,128)(2,1)} %bitcast.59) | data formatting | bytes 4194304 | tf_op jit(solution)/shard_map/dot_general | solution.py:100
  48.4 1.9 collective-permute-done.2
  50.5 0.2 fusion.10
  50.7 0.2 fusion.12
  50.9 0.8 fusion.15
  52.0 0.5 convolution_convert_fusion.1
  52.5 0.7 copy-done.8
  53.3 0.2 copy-done.9
  53.6 2.9 %gather_fusion = bf16[64,132,256]{2,1,0:T(8,128)(2,1)} fusion(bf16[16,132,256]{2,1,0:T(8,128)(2,1)S(1)} %pad_maximum_fusion.1, s32[1024]{0:T(1024)S(1)} %get-tuple-element.68), kind=kCustom, calls=%fused_computation | custom fusion | bytes 8651008 | tf_op jit(solution)/shard_map/gather | solution.py:78
  56.5 2.9 %gather_fusion.1 = bf16[64,132,256]{2,1,0:T(8,128)(2,1)} fusion(bf16[16,132,256]{2,1,0:T(8,128)(2,1)S(1)} %pad_maximum_fusion, s32[1024]{0:T(1024)S(1)} %get-tuple-element.68), kind=kCustom, calls=%fused_computation.1 | custom fusion | bytes 8651008 | tf_op jit(solution)/shard_map/gather | solution.py:78
  59.3 7.7 %broadcast_select_fusion = (bf16[64,132,256]{2,1,0:T(8,128)(2,1)}, bf16[64,132,256]{2,1,0:T(8,128)(2,1)}) fusion(bf16[64,132,256]{2,1,0:T(8,128)(2,1)} %gather_fusion.1, pred[64]{0:T(512)(128)(4,1)S(1)} %broadcast_compare_fusion, bf16[64,132,256]{2,1,0:T(8,128)(2,1)} %gather_fusion), kind=kLoop, calls=%fused_computation.8 | loop fusion | flops 4325376 | bytes 17301568 | tf_op jit(solution)/shard_map/jit(_where)/select_n | solution.py:78
  67.0 4.6 %all-to-all-start.1 = ((bf16[64,132,256]{2,1,0:T(8,128)(2,1)}), bf16[64,132,256]{2,1,0:T(8,128)(2,1)}, u32[]{:S(2)}, u32[]{:S(2)}) async-start(bf16[64,132,256]{2,1,0:T(8,128)(2,1)} %get-tuple-element.62), calls=%async_computation.2 | async-start | bytes 8912896 | tf_op jit(solution)/shard_map/all_to_all | solution.py:153
  71.6 11.3 %copy.81 = bf16[1024,4096]{1,0:T(8,128)(2,1)} copy(bf16[1024,4096]{0,1:T(8,128)(2,1)} %bitcast.57) | data formatting | bytes 16777216 | tf_op jit(solution)/shard_map/dot_general | solution.py:96
  83.0 1.2 reshape.513
  84.1 0.4 reshape.511
  84.5 6.1 %fusion.13 = f32[4,16,8,128]{3,1,2,0:T(8,128)S(1)} fusion(bf16[8,128,4096,1]{2,1,0,3:T(8,128)(2,1)} %bitcast.58, bf16[4,16,4096]{2,1,0:T(8,128)(2,1)S(1)} %copy-done.5), kind=kOutput, calls=%fused_computation.27 | convolution fusion | flops 536870912 | bytes 9175040 | tf_op jit(solution)/shard_map/dot_general | solution.py:96
  90.7 0.2 subtract_convert_fusion
  90.9 1.1 fusion.35
  92.0 31.5 %all-to-all-done.1 = bf16[64,132,256]{2,1,0:T(8,128)(2,1)} async-done(((bf16[64,132,256]{2,1,0:T(8,128)(2,1)}), bf16[64,132,256]{2,1,0:T(8,128)(2,1)}, u32[]{:S(2)}, u32[]{:S(2)}) %all-to-all-start.1) | async-done | bytes 4325408 | tf_op jit(solution)/shard_map/all_to_all | solution.py:153
  123.5 4.6 %all-to-all-start.2 = ((bf16[64,132,256]{2,1,0:T(8,128)(2,1)}), bf16[64,132,256]{2,1,0:T(8,128)(2,1)}, u32[]{:S(2)}, u32[]{:S(2)}) async-start(bf16[64,132,256]{2,1,0:T(8,128)(2,1)} %get-tuple-element.61), calls=%async_computation.3 | async-start | bytes 8912896 | tf_op jit(solution)/shard_map/all_to_all | solution.py:154
  128.1 0.5 fusion.7
  128.8 6.0 %fusion.1 = f32[4,16,4096]{2,1,0:T(8,128)} fusion(bf16[4,16,1024]{2,1,0:T(8,128)(2,1)S(1)} %dot_general.37, bf16[1024,4096]{1,0:T(8,128)(2,1)} %param.20), kind=kOutput, calls=%fused_computation.6 | convolution fusion | flops 536870912 | bytes 9568256 | tf_op jit(solution)/shard_map/dot_general | solution.py:137
  134.8 0.8 gather_fusion.2
  135.8 27.4 %reduce-scatter.2.cloned.1.call-done = f32[4,16,1024]{2,1,0:T(8,128)} async-done(((f32[4,16,4096]{2,1,0:T(8,128)}), f32[4,16,1024]{2,1,0:T(8,128)}) %reduce-scatter.2.cloned.1.call-update) | async-done | bytes 262160 | tf_op jit(solution)/shard_map/reduce_scatter | solution.py:140
  163.1 1.7 multiply_reduce_fusion
  164.9 9.3 %all-reduce.1 = (f32[4,16]{1,0:T(4,128)S(1)}, f32[4,16]{1,0:T(4,128)S(1)}) all-reduce(f32[4,16]{1,0:T(4,128)S(1)} %get-tuple-element.41, f32[4,16]{1,0:T(4,128)S(1)} %get-tuple-element.40), channel_id=1, replica_groups=mesh['dom'=8,'tp'=4] {'tp'}, use_global_device_ids=true, to_apply=%region_12.13 | all-reduce | flops 128 | bytes 1024 | tf_op jit(solution)/shard_map/psum | solution.py:143
  174.2 0.6 fusion.33
  174.8 12.4 %pmax.7 = f32[]{:T(128)} all-reduce(f32[]{:T(128)} %get-tuple-element.52), channel_id=1, replica_groups=mesh['dom'=8,'tp'=4] {'dom'}, use_global_device_ids=true, to_apply=%region_17.18 | all-reduce | flops 1 | bytes 8 | tf_op jit(solution)/shard_map/pmax | solution.py:149
  187.2 1.2 exponential_reduce_fusion
  188.4 12.5 %psum.23 = f32[]{:T(128)} all-reduce(f32[]{:T(128)} %exponential_reduce_fusion), channel_id=1, replica_groups=mesh['dom'=8,'tp'=4] {'dom'}, use_global_device_ids=true, to_apply=%region_19.20 | all-reduce | flops 1 | bytes 8 | tf_op jit(solution)/shard_map/psum | solution.py:150
  202.3 0.5 broadcast_subtract_fusion
  202.9 7.6 %scatter_fusion = bf16[16,132,256]{2,1,0:T(8,128)(2,1)S(1)} fusion(bf16[16,132,256]{2,1,0:T(8,128)(2,1)S(1)} %broadcast.505.clone, s32[64]{0:T(128)S(1)} %fusion.29, bf16[64,132,256]{2,1,0:T(8,128)(2,1)} %all-to-all-done.1), kind=kCustom, calls=%fused_computation.3 | custom fusion | bytes 12976384 | tf_op jit(solution)/shard_map/scatter | solution.py:82
  210.4 1.2 copy.66
  211.7 7.6 %scatter_fusion.1 = bf16[16,132,256]{2,1,0:T(8,128)(2,1)S(1)} fusion(bf16[16,132,256]{2,1,0:T(8,128)(2,1)S(1)} %broadcast.505.clone.1, s32[64]{0:T(128)S(1)} %fusion.29, bf16[64,132,256]{2,1,0:T(8,128)(2,1)} %all-to-all-done.2), kind=kCustom, calls=%fused_computation.4 | custom fusion | bytes 12976384 | tf_op jit(solution)/shard_map/scatter | solution.py:82
  219.3 1.2 copy.67
  (70 shorter events, 1.7 us)
Async XLA Ops:
  7.2 44.8 %copy-start = (bf16[4096,256]{1,0:T(8,128)(2,1)S(1)}, bf16[4096,256]{1,0:T(8,128)(2,1)}, u32[]{:S(2)}) copy-start(bf16[4096,256]{1,0:T(8,128)(2,1)} %param.19) | copy-start | bytes 6291460
  7.2 28.6 %collective-permute-start = (bf16[4,16,1024]{2,1,0:T(8,128)(2,1)}, bf16[4,16,1024]{2,1,0:T(8,128)(2,1)S(1)}, u32[]{:S(2)}, u32[]{:S(2)}) collective-permute-start(bf16[4,16,1024]{2,1,0:T(8,128)(2,1)} %param.15), channel_id=1, source_target_pairs={{0,1},{1,2},{2,3},{3,0},{4,5},{5,6},{6,7},{7,4},{8,9},{9,10},{10,1... | collective-permute-start | bytes 393224 | tf_op jit(solution)/shard_map/ppermute | solution.py:86
  24.4 42.6 %all-to-all-start = ((bf16[8,8,1]{1,2,0:T(2,128)(2,1)}), bf16[8,8,1]{1,2,0:T(2,128)(2,1)S(1)}, u32[]{:S(2)}, u32[]{:S(2)}) async-start(bf16[8,8,1]{1,2,0:T(2,128)(2,1)} %fusion.23), calls=%async_computation.1 | async-start | bytes 8192 | tf_op jit(solution)/shard_map/all_to_all | solution.py:155
  35.7 7.8 %collective-permute-start.1 = (bf16[4,16,1024]{2,1,0:T(8,128)(2,1)S(1)}, bf16[4,16,1024]{2,1,0:T(8,128)(2,1)S(1)}, u32[]{:S(2)}, u32[]{:S(2)}) collective-permute-start(bf16[4,16,1024]{2,1,0:T(8,128)(2,1)S(1)} %collective-permute-done), channel_id=1, source_target_pairs={{0,1},{1,2},{2,3},{3,0},{4,5},{5,6},{6,7},{7,4},{8,9},{9,10},{10,1... | collective-permute-start | bytes 393224 | tf_op jit(solution)/shard_map/ppermute | solution.py:86
  43.5 6.8 %collective-permute-start.2 = (bf16[4,16,1024]{2,1,0:T(8,128)(2,1)S(1)}, bf16[4,16,1024]{2,1,0:T(8,128)(2,1)S(1)}, u32[]{:S(2)}, u32[]{:S(2)}) collective-permute-start(bf16[4,16,1024]{2,1,0:T(8,128)(2,1)S(1)} %collective-permute-done.1), channel_id=1, source_target_pairs={{0,1},{1,2},{2,3},{3,0},{4,5},{5,6},{6,7},{7,4},{8,9},{9,10},{10,1... | collective-permute-start | bytes 393224 | tf_op jit(solution)/shard_map/ppermute | solution.py:86
  44.2 6.2 %copy-start.6 = (bf16[4,16,1024]{2,1,0:T(8,128)(2,1)S(1)}, bf16[4,16,1024]{2,1,0:T(8,128)(2,1)}, u32[]{:S(2)}) copy-start(bf16[4,16,1024]{2,1,0:T(8,128)(2,1)} %param.15) | copy-start | bytes 393220
  48.3 2.3 %copy-start.10 = (f32[4096]{0:T(1024)S(1)}, f32[4096]{0:T(1024)}, u32[]{:S(2)}) copy-start(f32[4096]{0:T(1024)} %param.16) | copy-start | bytes 49156
  48.4 2.5 %copy-start.3 = (bf16[256,4096]{1,0:T(8,128)(2,1)S(1)}, bf16[256,4096]{1,0:T(8,128)(2,1)}, u32[]{:S(2)}) copy-start(bf16[256,4096]{1,0:T(8,128)(2,1)} %copy.75) | copy-start | bytes 6291460
  50.9 1.1 copy-start.4
  52.0 1.2 copy-start.8
  52.0 1.5 copy-start.9
  67.0 56.5 %all-to-all-start.1 = ((bf16[64,132,256]{2,1,0:T(8,128)(2,1)}), bf16[64,132,256]{2,1,0:T(8,128)(2,1)}, u32[]{:S(2)}, u32[]{:S(2)}) async-start(bf16[64,132,256]{2,1,0:T(8,128)(2,1)} %get-tuple-element.62), calls=%async_computation.2 | async-start | bytes 8912896 | tf_op jit(solution)/shard_map/all_to_all | solution.py:153
  83.0 1.5 copy-start.5
  84.5 6.4 %copy-start.7 = (bf16[16,132,2,128]{3,2,1,0:T(2,128)(2,1)S(1)}, bf16[16,132,2,128]{3,2,1,0:T(2,128)(2,1)}, u32[]{:S(2)}) copy-start(bf16[16,132,2,128]{3,2,1,0:T(2,128)(2,1)} %reshape.513) | copy-start | bytes 3244036
  123.5 88.1 %all-to-all-start.2 = ((bf16[64,132,256]{2,1,0:T(8,128)(2,1)}), bf16[64,132,256]{2,1,0:T(8,128)(2,1)}, u32[]{:S(2)}, u32[]{:S(2)}) async-start(bf16[64,132,256]{2,1,0:T(8,128)(2,1)} %get-tuple-element.61), calls=%async_computation.3 | async-start | bytes 8912896 | tf_op jit(solution)/shard_map/all_to_all | solution.py:154
  128.1 35.0 %reduce-scatter.2.cloned.1.call-start = ((), (), s32[]{:S(2)}) async-start(), calls=%async_computation.4 | async-start | bytes 1310720 | tf_op jit(solution)/shard_map/reduce_scatter | solution.py:140
  128.7 6.0 %copy-start.2 = (bf16[128256]{0:T(1024)(128)(2,1)S(1)}, bf16[128256]{0:T(1024)(128)(2,1)}, u32[]{:S(2)}) copy-start(bf16[128256]{0:T(1024)(128)(2,1)} %param.24) | copy-start | bytes 769540
  134.7 28.4 %copy-start.11 = (f32[1024]{0:T(1024)S(1)}, f32[1024]{0:T(1024)}, u32[]{:S(2)}) copy-start(f32[1024]{0:T(1024)} %param.25) | copy-start | bytes 12292
  134.7 39.4 %copy-start.12 = (f32[16]{0:T(128)S(1)}, f32[16]{0:T(128)}, u32[]{:S(2)}) copy-start(f32[16]{0:T(128)} %param.26) | copy-start | bytes 196
  211.7 8.8 %copy-start.1 = (bf16[4096,256]{1,0:T(8,128)(2,1)S(1)}, bf16[4096,256]{1,0:T(8,128)(2,1)}, u32[]{:S(2)}) copy-start(bf16[4096,256]{1,0:T(8,128)(2,1)} %param.19) | copy-start | bytes 6291460
Sparse Core Ops, SparseCore 0:
  134.9 28.1 reduce-scatter.1
